TPU v7x, 32 devices: a whole 2x2x4 slice. The times are simulated.
32 devices in a mesh: section: 4 (over y, x), fsdp: 8 (over z, core).
Axes of the slice: x: 2, y: 2, z: 4, core: 2. Of those that a mesh axis runs over, the one named last changes fastest.
Arguments:
- master: float32 [4, 64, 4096], P('section', 'fsdp'), may hold values from -0.12 to 0.12
- first_moment: float32 [4, 64, 4096], P('section', 'fsdp'), may hold values from -0.2 to 0.2
- second_moment: float32 [4, 64, 4096], P('section', 'fsdp'), may hold values from 0.25 to 1
- gradient: float32 [4, 64, 4096], P('section', 'fsdp'), may hold values from -64 to 64
Outputs:
- new_master: float32 [4, 64, 4096], P('section', 'fsdp')
- new_first: float32 [4, 64, 4096], P('section', 'fsdp')
- new_second: float32 [4, 64, 4096], P('section', 'fsdp')
- weights: bfloat16 [4, 64, 4096], P('section')
- grad_rms: float32 [], replicated
All inputs are finite; a program needn't handle non-finite values.
Results may differ from a plain program's by a relative error of at most 0.001.
Values may be sent and summed in bfloat16 or wider, within the bound.
A program may use at most 64 MiB of HBM per device.

v0:
```python
import jax
import jax.numpy as jnp
from jax import lax
from jax.sharding import PartitionSpec as P

BETA_ONE = 0.9
BETA_TWO = 0.95
LEARN_RATE = 0.05
DECAY = 0.1
EPSILON = 1e-08
BIAS_STEPS = 10.0


def adamw_part(master, first_moment, second_moment, gradient, clip_scale):
    scaled = clip_scale * gradient
    new_first = BETA_ONE * first_moment + (1.0 - BETA_ONE) * scaled
    new_second = BETA_TWO * second_moment + (1.0 - BETA_TWO) * scaled * scaled
    first_hat = new_first / (1.0 - BETA_ONE**BIAS_STEPS)
    second_hat = new_second / (1.0 - BETA_TWO**BIAS_STEPS)
    update = first_hat / (jnp.sqrt(second_hat) + EPSILON)
    new_master = master * (1.0 - LEARN_RATE * DECAY) - LEARN_RATE * update
    return (new_master, new_first, new_second)


def local(master, first_moment, second_moment, gradient):
    partial_sq = jnp.sum(gradient * gradient)
    within = lax.psum(partial_sq, "fsdp")
    squares = lax.psum(within, "section")
    grad_norm = jnp.sqrt(squares)
    param_count = float(
        lax.axis_size("section")
        * lax.axis_size("fsdp")
        * gradient.shape[0]
        * gradient.shape[1]
        * gradient.shape[2]
    )
    limit = jnp.float32(0.5 * param_count**0.5)
    clip_scale = limit / jnp.maximum(grad_norm, limit)
    grad_rms = grad_norm / jnp.float32(param_count**0.5)
    new_master, new_first, new_second = adamw_part(
        master, first_moment, second_moment, gradient, clip_scale
    )
    weights = lax.all_gather(new_master.astype(jnp.bfloat16), "fsdp", axis=1, tiled=True)
    return (new_master, new_first, new_second, weights, grad_rms)


def solution(mesh):
    placed = (
        P("section", "fsdp", None),
        P("section", "fsdp", None),
        P("section", "fsdp", None),
        P("section", "fsdp", None),
    )
    return jax.shard_map(
        local,
        mesh=mesh,
        in_specs=placed,
        out_specs=(
            P("section", "fsdp", None),
            P("section", "fsdp", None),
            P("section", "fsdp", None),
            P("section", None, None),
            P(),
        ),
        check_vma=False,
    )
```

profile of v0, /device:TPU:0, one launch (start us, length us, event | category | flops | bytes accessed | tf_op | source)
XLA Modules:
  0.0 50.9 jit_solution(5301626764726928907)
XLA Ops:
  0.6 0.0 copy-start
  0.6 1.6 %multiply_reduce_fusion = f32[]{:T(128)} fusion(f32[1,8,4096]{2,1,0:T(8,128)} %param.7), kind=kLoop, calls=%fused_computation.4 | loop fusion | flops 65535 | bytes 131076 | tf_op jit(solution)/shard_map/reduce_sum | solution.py:26
  2.2 18.7 %psum.14 = f32[]{:T(128)} all-reduce(f32[]{:T(128)} %multiply_reduce_fusion), channel_id=1, replica_groups=mesh['section'=4,'fsdp'=8] {'fsdp'}, use_global_device_ids=true, to_apply=%region_1.0 | all-reduce | flops 1 | bytes 8 | tf_op jit(solution)/shard_map/psum | solution.py:27
  21.0 10.5 %psum.15 = f32[]{:T(128)} all-reduce(f32[]{:T(128)} %psum.14), channel_id=1, replica_groups=mesh['section'=4,'fsdp'=8] {'section'}, use_global_device_ids=true, to_apply=%region_2.0 | all-reduce | flops 1 | bytes 8 | tf_op jit(solution)/shard_map/psum | solution.py:28
  32.2 0.0 copy-done
  32.2 1.8 %fusion.1 = (bf16[1,8,4096]{2,1,0:T(8,128)(2,1)S(1)}, f32[1,8,4096]{2,1,0:T(8,128)}, f32[1,8,4096]{2,1,0:T(8,128)}, f32[1,8,4096]{2,1,0:T(8,128)}) fusion(f32[1,8,4096]{2,1,0:T(8,128)} %param.4, f32[1,8,4096]{2,1,0:T(8,128)S(1)} %copy-done, f32[]{:T(128)S(6)} %div.21, f32[1,8,4096]{2,1,0:T(8,128)} %param.5, f32[1,8,4096]{2,1,0:T(8,128)} %param.6), kind=kLoop, calls=%fused_computation.5 | loop fusion | flops 524288 | bytes 983044 | tf_op jit(solution)/shard_map/convert_element_type | solution.py:43
  34.1 14.9 %all_gather.3 = bf16[1,64,4096]{2,1,0:T(8,128)(2,1)S(1)} all-gather(bf16[1,8,4096]{2,1,0:T(8,128)(2,1)S(1)} %get-tuple-element.5), channel_id=1, replica_groups=mesh['section'=4,'fsdp'=8] {'fsdp'}, dimensions={1}, use_global_device_ids=true | all-gather | bytes 589824 | tf_op jit(solution)/shard_map/all_gather | solution.py:43
  49.0 0.8 %copy.10 = bf16[1,64,4096]{2,1,0:T(8,128)(2,1)} copy(bf16[1,64,4096]{2,1,0:T(8,128)(2,1)S(1)} %all_gather.3) | data formatting | bytes 1048576
Async XLA Ops:
  0.6 31.6 %copy-start = (f32[1,8,4096]{2,1,0:T(8,128)S(1)}, f32[1,8,4096]{2,1,0:T(8,128)}, u32[]{:S(2)}) copy-start(f32[1,8,4096]{2,1,0:T(8,128)} %param.7) | copy-start | bytes 393220
where the time goes:
time: 51.1 us; the launch traced here: 50.9 us
  blocking collectives  44.2 us (86%)
  other arithmetic  3.44 us (7%)
  between operations  2.51 us (5%)
  local copies, waits for them, and re-layouts  0.8 us (2%)
    psum x1, blocking collectives, local(): within = lax.psum(partial_sq, 'fsdp')  18.7 us
    all_gather x1, blocking collectives, local(): lax.all_gather(new_master.astype(jnp.bfloat16), 'fsdp', axis=1, tiled=True)  14.9 us
    psum x1, blocking collectives, local(): squares = lax.psum(within, 'section')  10.5 us
    convert_element_type x1, other arithmetic, local(): new_master.astype(jnp.bfloat16)  1.83 us
    reduce_sum x1, other arithmetic, local(): partial_sq = jnp.sum(gradient * gradient)  1.61 us

commit v1 on v0

--- a/solution.py
+++ b/solution.py
@@ -25,7 +25,7 @@
 def local(master, first_moment, second_moment, gradient):
     partial_sq = jnp.sum(gradient * gradient)
     within = lax.psum(partial_sq, "fsdp")
-    squares = lax.psum(within, "section")
+    squares = lax.all_gather(within, "section").sum(axis=0)
     grad_norm = jnp.sqrt(squares)
     param_count = float(
         lax.axis_size("section")

time: 51.1 us -> 53.1 us (1.039)
  local copies, waits for them, and re-layouts: 0.8 us -> 2.79 us
  blocking collectives: 44.2 us -> 43.5 us
  other arithmetic: 3.44 us -> 4.04 us
    psum x1 -> x0, blocking collectives: 10.5 us -> none  [local(): squares = lax.psum(within, 'section')]
    unnamed x0 -> x1, blocking collectives: none -> 9.88 us
    unnamed x3 -> x8, local copies, waits for them, and re-layouts: 0.8 us -> 2.79 us
    reduce_sum x0 -> x1, other arithmetic: none -> 0.6 us  [local(): squares = lax.all_gather(within, 'section').sum(axis=0)]
where the time goes in v1:
time: 53.1 us; the launch traced here: 52.9 us
  blocking collectives  43.5 us (82%)
  other arithmetic  4.04 us (8%)
  local copies, waits for them, and re-layouts  2.79 us (5%)
  between operations  2.52 us (5%)
    psum x1, blocking collectives, local(): within = lax.psum(partial_sq, 'fsdp')  18.7 us
    all_gather x1, blocking collectives, local(): lax.all_gather(new_master.astype(jnp.bfloat16), 'fsdp', axis=1, tiled=True)  14.9 us
    unnamed x1, blocking collectives  9.88 us
    unnamed x8, local copies, waits for them, and re-layouts  2.79 us
    convert_element_type x1, other arithmetic, local(): new_master.astype(jnp.bfloat16)  1.83 us
    reduce_sum x1, other arithmetic, local(): partial_sq = jnp.sum(gradient * gradient)  1.6 us

profile of v1, /device:TPU:0, one launch (start us, length us, event | category | flops | bytes accessed | tf_op | source)
XLA Modules:
  0.0 52.9 jit_solution(12788073690955085228)
XLA Ops:
  0.6 0.0 copy-start
  0.6 1.6 %multiply_reduce_fusion = f32[]{:T(128)} fusion(f32[1,8,4096]{2,1,0:T(8,128)} %param.7), kind=kLoop, calls=%fused_computation.4 | loop fusion | flops 65535 | bytes 131076 | tf_op jit(solution)/shard_map/reduce_sum | solution.py:26
  2.2 0.0 copy-start.1
  2.2 18.7 %psum.7 = f32[1]{0:T(128)} all-reduce(f32[1]{0:T(128)} %bitcast), channel_id=1, replica_groups=mesh['section'=4,'fsdp'=8] {'fsdp'}, use_global_device_ids=true, to_apply=%region_1.0 | all-reduce | flops 1 | bytes 8 | tf_op jit(solution)/shard_map/psum | solution.py:27
  21.0 0.0 copy-done.1
  21.0 0.6 %dynamic-slice = u32[1]{0:T(128)} dynamic-slice(u32[32]{0:T(128)S(1)} %copy-done.1, u32[]{:T(128)S(6)} %add.18), dynamic_slice_sizes={1} | dynamic-slice | bytes 12
  21.6 1.4 %dynamic-update-slice = f32[4]{0:T(128)S(1)} dynamic-update-slice(f32[4]{0:T(128)S(1)} %broadcast.6, f32[1]{0:T(128)} %psum.7, u32[]{:T(128)} %bitcast.1) | dynamic-update-slice | bytes 12
  23.0 9.9 %all-reduce = f32[4]{0:T(128)S(1)} all-reduce(f32[4]{0:T(128)S(1)} %dynamic-update-slice), channel_id=1, replica_groups=mesh['section'=4,'fsdp'=8] {'section'}, use_global_device_ids=true, to_apply=%add | all-reduce | flops 4 | bytes 32
  32.8 0.6 %reduce_sum.19 = f32[]{:T(128)} reduce(f32[4]{0:T(128)S(1)} %all-reduce, f32[]{:T(128)} %constant.6.clone.1), dimensions={0}, to_apply=%region_2.0 | reduce | flops 3 | bytes 24 | tf_op jit(solution)/shard_map/reduce_sum | solution.py:28
  34.2 0.0 copy-done
  34.2 1.8 %fusion.1 = (bf16[1,8,4096]{2,1,0:T(8,128)(2,1)S(1)}, f32[1,8,4096]{2,1,0:T(8,128)}, f32[1,8,4096]{2,1,0:T(8,128)}, f32[1,8,4096]{2,1,0:T(8,128)}) fusion(f32[1,8,4096]{2,1,0:T(8,128)} %param.4, f32[1,8,4096]{2,1,0:T(8,128)S(1)} %copy-done, f32[]{:T(128)S(6)} %div.21, f32[1,8,4096]{2,1,0:T(8,128)} %param.5, f32[1,8,4096]{2,1,0:T(8,128)} %param.6), kind=kLoop, calls=%fused_computation.5 | loop fusion | flops 524288 | bytes 983044 | tf_op jit(solution)/shard_map/convert_element_type | solution.py:43
  36.0 14.9 %all_gather.11 = bf16[1,64,4096]{2,1,0:T(8,128)(2,1)S(1)} all-gather(bf16[1,8,4096]{2,1,0:T(8,128)(2,1)S(1)} %get-tuple-element.5), channel_id=1, replica_groups=mesh['section'=4,'fsdp'=8] {'fsdp'}, dimensions={1}, use_global_device_ids=true | all-gather | bytes 589824 | tf_op jit(solution)/shard_map/all_gather | solution.py:43
  50.9 0.8 %copy.11 = bf16[1,64,4096]{2,1,0:T(8,128)(2,1)} copy(bf16[1,64,4096]{2,1,0:T(8,128)(2,1)S(1)} %all_gather.11) | data formatting | bytes 1048576
  (1 shorter events, 0.0 us)
Async XLA Ops:
  0.6 33.5 %copy-start = (f32[1,8,4096]{2,1,0:T(8,128)S(1)}, f32[1,8,4096]{2,1,0:T(8,128)}, u32[]{:S(2)}) copy-start(f32[1,8,4096]{2,1,0:T(8,128)} %param.7) | copy-start | bytes 393220
  2.2 18.7 %copy-start.1 = (u32[32]{0:T(128)S(1)}, u32[32]{0:T(128)}, u32[]{:S(2)}) copy-start(u32[32]{0:T(128)} %constant.31) | copy-start | bytes 388
